TPU v7x, 32 devices: a whole 2x2x4 slice. The times are simulated.
32 devices in a mesh: rep: 8 (over z, core), tp: 4 (over y, x).
Axes of the slice: x: 2, y: 2, z: 4, core: 2. Of those that a mesh axis runs over, the one named last changes fastest.
Arguments:
- queries: bfloat16 [64, 8192], P('rep', 'tp'), may hold values from -200 to 200
- new_keys: bfloat16 [64, 1024], P('rep', 'tp'), may hold values from -6 to 6
- new_values: bfloat16 [64, 1024], P('rep', 'tp'), may hold values from -6 to 6
- key_pool: bfloat16 [768, 128, 1024], P('rep', 'tp'), may hold values from -6 to 6
- value_pool: bfloat16 [768, 128, 1024], P('rep', 'tp'), may hold values from -6 to 6
- lengths: int32 [64], replicated, may hold values from 1 to 1536, as said below
- page_table: int32 [64, 12], P('rep'), may hold values from -1 to 95, as said below
- mig_slot: int32 [8], replicated, may hold values from 0 to 7
- mig_dst: int32 [8], replicated, may hold values from 0 to 7, as said below
Outputs:
- attended: bfloat16 [64, 8192], P('rep', 'tp')
- moved_keys: bfloat16 [96, 128, 1024], P('rep', 'tp')
- moved_values: bfloat16 [96, 128, 1024], P('rep', 'tp')
Inputs may be any that keep to these rules, and one draw needn't show every extreme that they name: mig_dst[r] = (r + c) mod 8 for one offset c with 1 <= c < 8, the same for every replica. `page_table`: row q lists distinct pool pages of its replica for its first ceil(lengths[q] / 128) pages and -1 after them. `lengths`: some request has exactly 1536 cached tokens.
All inputs are finite; a program needn't handle non-finite values.
Results may differ from a plain program's by a relative error of at most 0.0065.
Values may be sent and summed in bfloat16 or wider, within the bound.
A program may use at most 64 MiB of HBM per device.

v0:
```python
import functools
import math


import jax
import jax.numpy as jnp
from jax import lax
from jax.experimental import pallas as pl
from jax.experimental.pallas import tpu as pltpu
from jax.sharding import PartitionSpec as P

H = 64
KVH = 8
DH = 128
LOW = -1e30


def route_by(count, distance):
    return [(i, (i + distance) % count) for i in range(count)]


def pick_kernel(
    table_ref, mig_ref, q_ref, nk_ref, nv_ref, key_ref, value_ref, row_ref, kout_ref, vout_ref, sems
):
    pages = kout_ref.shape[0]
    leaving = mig_ref[lax.axis_index("rep")]

    @pl.loop(0, pages)
    def _(j):
        page = jnp.maximum(table_ref[leaving, j], 0)
        pltpu.make_async_copy(key_ref.at[page], kout_ref.at[j], sems.at[0]).start()
        pltpu.make_async_copy(value_ref.at[page], vout_ref.at[j], sems.at[1]).start()

    at = 0
    for ref in (q_ref, nk_ref, nv_ref):
        width = ref.shape[1]
        slot = lax.broadcasted_iota(jnp.int32, ref.shape, 0)
        chosen = jnp.where(slot == leaving, ref[...].astype(jnp.float32), 0.0)
        row = jnp.sum(chosen, axis=0, keepdims=True)
        row_ref[:, at : at + width] = row.astype(jnp.bfloat16)
        at += width
    pltpu.make_async_copy(key_ref.at[pl.ds(0, pages)], kout_ref, sems.at[0]).wait()
    pltpu.make_async_copy(value_ref.at[pl.ds(0, pages)], vout_ref, sems.at[1]).wait()

    @pl.loop(0, pages)
    def _(j):
        @pl.when(table_ref[leaving, j] < 0)
        def _():
            kout_ref[j] = jnp.zeros(kout_ref.shape[1:], kout_ref.dtype)
            vout_ref[j] = jnp.zeros(vout_ref.shape[1:], vout_ref.dtype)


def picked(table, mig_slot, queries, new_keys, new_values, key_pool, value_pool):
    shape = (table.shape[1],) + key_pool.shape[1:]
    width = queries.shape[1] + 2 * new_keys.shape[1]
    return pl.pallas_call(
        pick_kernel,
        out_shape=[
            jax.ShapeDtypeStruct((1, width), jnp.bfloat16),
            jax.ShapeDtypeStruct(shape, key_pool.dtype),
            jax.ShapeDtypeStruct(shape, key_pool.dtype),
        ],
        in_specs=[pl.BlockSpec(memory_space=pltpu.SMEM)] * 2
        + [pl.BlockSpec(memory_space=pltpu.VMEM)] * 3
        + [pl.BlockSpec(memory_space=pl.ANY)] * 2,
        out_specs=[pl.BlockSpec(memory_space=pltpu.VMEM)] * 3,
        scratch_shapes=[pltpu.SemaphoreType.DMA((2,))],
        compiler_params=pltpu.CompilerParams(vmem_limit_bytes=8 << 20),
        cost_estimate=pl.CostEstimate(
            flops=0, bytes_accessed=8 * math.prod(shape), transcendentals=0
        ),
    )(table, mig_slot, queries, new_keys, new_values, key_pool, value_pool)


def greet(parts):
    me = lax.axis_index("tp")
    barrier = pltpu.get_barrier_semaphore()
    for k in range(1, parts):
        pl.semaphore_signal(
            barrier,
            inc=1,
            device_id={"tp": lax.rem(me + k, parts)},
            device_id_type=pl.DeviceIdType.MESH,
        )
    pl.semaphore_wait(barrier, parts - 1)
    return me


def share_kernel(mig_ref, back_ref, tokens_ref, all_ref, mine_ref, own, send_sems, recv_sems):
    parts, slots, heads_here, _ = all_ref.shape
    chunks = tokens_ref.shape[1]
    leaving = mig_ref[lax.axis_index("rep")]
    back = back_ref[...].astype(jnp.float32)
    row = jnp.concatenate([back[:, h * DH : (h + 1) * DH] for h in range(chunks)], axis=0)
    for i in range(slots):
        value = jnp.where(leaving == i, row, tokens_ref[i].astype(jnp.float32))
        value = value.astype(jnp.bfloat16)
        mine_ref[i] = value
        own[i] = value[:heads_here]
    me = greet(parts)
    copies = []
    for k in range(1, parts):
        copy = pltpu.make_async_remote_copy(
            src_ref=own,
            dst_ref=all_ref.at[me],
            send_sem=send_sems.at[k - 1],
            recv_sem=recv_sems.at[k - 1],
            device_id={"tp": lax.rem(me + k, parts)},
            device_id_type=pl.DeviceIdType.MESH,
        )
        copy.start()
        copies.append(copy)
    all_ref[me] = own[...]
    for copy in copies:
        copy.wait()


def shared(mig_slot, back, tokens, heads_here, parts):
    slots = tokens.shape[0]
    return pl.pallas_call(
        share_kernel,
        out_shape=[
            jax.ShapeDtypeStruct((parts, slots, heads_here, DH), jnp.bfloat16),
            jax.ShapeDtypeStruct(tokens.shape, jnp.bfloat16),
        ],
        in_specs=[pl.BlockSpec(memory_space=pltpu.SMEM)]
        + [pl.BlockSpec(memory_space=pltpu.VMEM)] * 2,
        out_specs=[pl.BlockSpec(memory_space=pltpu.VMEM)] * 2,
        scratch_shapes=[
            pltpu.VMEM((slots, heads_here, DH), jnp.bfloat16),
            pltpu.SemaphoreType.DMA((parts - 1,)),
            pltpu.SemaphoreType.DMA((parts - 1,)),
        ],
        compiler_params=pltpu.CompilerParams(
            collective_id=0, has_side_effects=True, vmem_limit_bytes=8 << 20
        ),
        cost_estimate=pl.CostEstimate(flops=0, bytes_accessed=8 << 20, transcendentals=0),
    )(mig_slot, back, tokens)


def flat_rows(block):
    pages, rows, width = block.shape
    if rows % 16 == 0:
        return block.reshape(pages * rows, width)
    return block.astype(jnp.float32).reshape(pages * rows, width).astype(block.dtype)


def attend_kernel(
    table_ref,
    len_ref,
    start_ref,
    q_ref,
    key_ref,
    value_ref,
    out_ref,
    kbuf,
    vbuf,
    stats_ref,
    ksem,
    vsem,
):
    slots, pages, rows, width = kbuf.shape
    parts, heads_here = q_ref.shape[0], q_ref.shape[2]
    group = H // KVH
    page_len = rows * parts
    scaling = 1.0 / math.sqrt(DH)
    steps = 3 if pages % 3 == 0 else 1
    step_pages = pages // steps

    def live_pages(i):
        return lax.div(len_ref[i] + (page_len - 1), page_len)

    def key_copy(i, j):
        page = jnp.maximum(table_ref[i, j], 0)
        return pltpu.make_async_copy(key_ref.at[page], kbuf.at[i, j], ksem.at[i, j])

    def value_copy(i, j):
        page = jnp.maximum(table_ref[i, j], 0)
        return pltpu.make_async_copy(value_ref.at[page], vbuf.at[i, j], vsem.at[i, j])

    @pl.loop(0, slots)
    def _(i):
        @pl.loop(0, live_pages(i))
        def _(j):
            key_copy(i, j).start()
            value_copy(i, j).start()

    head = lax.broadcasted_iota(jnp.int32, (H, DH), 0) // group
    column = lax.broadcasted_iota(jnp.int32, (H, DH), 1)
    stats_ref[...] = jnp.zeros_like(stats_ref)

    def attend(i, used):
        tokens = used * rows
        lane = lax.broadcasted_iota(jnp.int32, (H, tokens), 1)
        position = (lane // rows) * page_len + lane % rows + start_ref[0]
        q = jnp.concatenate([q_ref[t, i].astype(jnp.float32) for t in range(parts)], axis=0)
        spread = jnp.concatenate(
            [jnp.where(head == g, q, 0.0).astype(jnp.bfloat16) for g in range(KVH)], axis=1
        )
        scores = lax.dot_general(
            spread,
            flat_rows(kbuf[i, 0:used]),
            (((1,), (1,)), ((), ())),
            preferred_element_type=jnp.float32,
        )
        usable = position < len_ref[i]
        masked = jnp.where(usable, scores * scaling, LOW)
        peak = jnp.max(masked, axis=1, keepdims=True)
        weights = jnp.where(usable, jnp.exp(masked - peak), 0.0)
        total = jnp.sum(weights, axis=1, keepdims=True)
        mixed = jnp.dot(
            weights.astype(jnp.bfloat16),
            flat_rows(vbuf[i, 0:used]),
            preferred_element_type=jnp.float32,
        )
        own = jnp.concatenate(
            [
                mixed[g * group : (g + 1) * group, g * DH : (g + 1) * DH]
                for g in range(KVH)
            ],
            axis=0,
        )
        for t in range(parts):
            out_ref[t, i] = own[t * heads_here : (t + 1) * heads_here]
        stats = jnp.where(column == i, peak, stats_ref[...])
        stats_ref[...] = jnp.where(column == i + slots, total, stats)

    @pl.loop(0, slots)
    def _(i):
        live = live_pages(i)
        needed = lax.div(live + (step_pages - 1), step_pages)

        @pl.loop(live, needed * step_pages)
        def _(j):
            vbuf[i, j] = jnp.zeros((rows, width), vbuf.dtype)

        @pl.loop(0, live)
        def _(j):
            key_copy(i, j).wait()
            value_copy(i, j).wait()

        for step in range(1, steps + 1):

            @pl.when(needed == step)
            def _():
                attend(i, step * step_pages)

    for t in range(parts):
        out_ref[t, slots] = stats_ref[t * heads_here : (t + 1) * heads_here]


def attended_parts(table, lens, start, q, key_pool, value_pool, parts):
    slots, pages = table.shape
    rows, width = key_pool.shape[1:]
    buffer = (slots, pages, rows, width)
    return pl.pallas_call(
        attend_kernel,
        out_shape=jax.ShapeDtypeStruct((parts, slots + 1, H // parts, DH), jnp.float32),
        in_specs=[pl.BlockSpec(memory_space=pltpu.SMEM)] * 3
        + [pl.BlockSpec(memory_space=pltpu.VMEM)]
        + [pl.BlockSpec(memory_space=pl.ANY)] * 2,
        out_specs=pl.BlockSpec(memory_space=pltpu.VMEM),
        scratch_shapes=[
            pltpu.VMEM(buffer, key_pool.dtype),
            pltpu.VMEM(buffer, value_pool.dtype),
            pltpu.VMEM((H, DH), jnp.float32),
            pltpu.SemaphoreType.DMA((slots, pages)),
            pltpu.SemaphoreType.DMA((slots, pages)),
        ],
        compiler_params=pltpu.CompilerParams(vmem_limit_bytes=24 << 20),
        cost_estimate=pl.CostEstimate(
            flops=4 * H * pages * rows * width * slots,
            bytes_accessed=4 * math.prod(buffer),
            transcendentals=0,
        ),
    )(table, lens, start, q, key_pool, value_pool)


def finish_kernel(
    mig_ref,
    part_ref,
    mine_ref,
    tk_ref,
    tv_ref,
    out_ref,
    leaver_ref,
    flat,
    landed,
    send_sems,
    recv_sems,
):
    parts, _, heads_here, _ = part_ref.shape
    slots = mine_ref.shape[0]
    repeat = heads_here // tk_ref.shape[1]
    leaving = mig_ref[lax.axis_index("rep")]
    scaling = 1.0 / math.sqrt(DH)
    me = greet(parts)
    copies = []
    for k in range(1, parts):
        peer = lax.rem(me + k, parts)
        copy = pltpu.make_async_remote_copy(
            src_ref=part_ref.at[peer],
            dst_ref=landed.at[k - 1],
            send_sem=send_sems.at[k - 1],
            recv_sem=recv_sems.at[k - 1],
            device_id={"tp": peer},
            device_id_type=pl.DeviceIdType.MESH,
        )
        copy.start()
        copies.append(copy)

    def spread(ref, i):
        value = ref[i].astype(jnp.float32)
        return jnp.concatenate(
            [
                jnp.broadcast_to(value[g : g + 1], (repeat, DH))
                for g in range(value.shape[0])
            ],
            axis=0,
        )

    fresh, values = [], []
    for i in range(slots):
        q = mine_ref[i].astype(jnp.float32)[:heads_here]
        fresh.append(jnp.sum(q * spread(tk_ref, i), axis=-1, keepdims=True) * scaling)
        values.append(spread(tv_ref, i))
    for copy in copies:
        copy.wait()
    stats = [part_ref[me, slots]] + [landed[k, slots] for k in range(parts - 1)]
    leaver = jnp.zeros((heads_here, DH), jnp.float32)
    for i in range(slots):
        top = fresh[i]
        for stat in stats:
            top = jnp.maximum(top, stat[:, i : i + 1])
        weight = jnp.exp(fresh[i] - top)
        total = weight
        mixed = weight.astype(jnp.bfloat16).astype(jnp.float32) * values[i]
        for k, stat in enumerate(stats):
            scale = jnp.exp(stat[:, i : i + 1] - top)
            block = part_ref[me, i] if k == 0 else landed[k - 1, i]
            total = total + scale * stat[:, slots + i : slots + i + 1]
            mixed = mixed + scale * block
        result = mixed / total
        leaver = jnp.where(leaving == i, result, leaver)
        for h in range(heads_here):
            flat[i : i + 1, h * DH : (h + 1) * DH] = result[h : h + 1]
    out_ref[...] = flat[...].astype(out_ref.dtype)
    row = jnp.concatenate([leaver[h : h + 1] for h in range(heads_here)], axis=1)
    leaver_ref[...] = row.astype(leaver_ref.dtype)


def finished(mig_slot, partials, mine, token_keys, token_values):
    parts, _, heads_here, _ = partials.shape
    slots = mine.shape[0]
    return pl.pallas_call(
        finish_kernel,
        out_shape=[
            jax.ShapeDtypeStruct((slots, heads_here * DH), jnp.bfloat16),
            jax.ShapeDtypeStruct((1, heads_here * DH), jnp.bfloat16),
        ],
        in_specs=[pl.BlockSpec(memory_space=pltpu.SMEM)]
        + [pl.BlockSpec(memory_space=pltpu.VMEM)] * 4,
        out_specs=[pl.BlockSpec(memory_space=pltpu.VMEM)] * 2,
        scratch_shapes=[
            pltpu.VMEM((slots, heads_here * DH), jnp.float32),
            pltpu.VMEM((parts - 1,) + partials.shape[1:], jnp.float32),
            pltpu.SemaphoreType.DMA((parts - 1,)),
            pltpu.SemaphoreType.DMA((parts - 1,)),
        ],
        compiler_params=pltpu.CompilerParams(
            collective_id=1, has_side_effects=True, vmem_limit_bytes=8 << 20
        ),
        cost_estimate=pl.CostEstimate(flops=0, bytes_accessed=8 << 20, transcendentals=0),
    )(mig_slot, partials, mine, token_keys, token_values)


def place_kernel(
    mig_ref, result_ref, row_ref, key_ref, value_ref, out_ref, kout_ref, vout_ref, kbuf, vbuf, sems
):
    pages = kbuf.shape[0]
    lanes = ((key_ref, kbuf, kout_ref), (value_ref, vbuf, vout_ref))
    span = 3 if pages % 3 == 0 else 1
    cuts = [pl.ds(j, span) for j in range(0, pages, span)]
    pairs = [(n, c) for c in range(len(cuts)) for n in range(2)]
    for n, c in pairs:
        source, buf, _ = lanes[n]
        pltpu.make_async_copy(source.at[cuts[c]], buf.at[cuts[c]], sems.at[n, c]).start()
    leaving = mig_ref[lax.axis_index("rep")]
    slot = lax.broadcasted_iota(jnp.int32, result_ref.shape, 0)
    row = row_ref[...].astype(jnp.float32)
    result = result_ref[...].astype(jnp.float32)
    out_ref[...] = jnp.where(slot == leaving, row, result).astype(out_ref.dtype)
    for n, c in pairs:
        source, buf, sink = lanes[n]
        pltpu.make_async_copy(source.at[cuts[c]], buf.at[cuts[c]], sems.at[n, c]).wait()
        pltpu.make_async_copy(buf.at[cuts[c]], sink.at[cuts[c]], sems.at[n, c]).start()
    for n, c in pairs:
        _, buf, sink = lanes[n]
        pltpu.make_async_copy(buf.at[cuts[c]], sink.at[cuts[c]], sems.at[n, c]).wait()


def placed_results(mig_slot, result, row, moved_keys, moved_values):
    moved = jax.ShapeDtypeStruct(moved_keys.shape, moved_keys.dtype)
    return pl.pallas_call(
        place_kernel,
        out_shape=[jax.ShapeDtypeStruct(result.shape, result.dtype), moved, moved],
        in_specs=[pl.BlockSpec(memory_space=pltpu.SMEM)]
        + [pl.BlockSpec(memory_space=pltpu.VMEM)] * 2
        + [pl.BlockSpec(memory_space=pl.ANY)] * 2,
        out_specs=[pl.BlockSpec(memory_space=pltpu.VMEM)]
        + [pl.BlockSpec(memory_space=pl.ANY)] * 2,
        scratch_shapes=[
            pltpu.VMEM(moved.shape, moved.dtype),
            pltpu.VMEM(moved.shape, moved.dtype),
            pltpu.SemaphoreType.DMA((2, moved.shape[0])),
        ],
        compiler_params=pltpu.CompilerParams(vmem_limit_bytes=8 << 20),
    )(mig_slot, result, row, moved_keys, moved_values)


def token_rows(fresh, parts, part_index):
    slots, width = fresh.shape
    heads_here = H // parts
    if width % DH == 0:
        return fresh.reshape(slots, width // DH, DH)
    every = lax.all_gather(fresh, "tp", axis=1, tiled=True).reshape(slots, KVH, DH)
    every = jnp.repeat(every, H // KVH, axis=1)
    return lax.dynamic_slice_in_dim(every, part_index * heads_here, heads_here, 1)


def body(
    queries, new_keys, new_values, key_pool, value_pool, lengths, page_table, mig_slot, mig_dst
):
    replicas = lax.axis_size("rep")
    parts = lax.axis_size("tp")
    here_rep = lax.axis_index("rep")
    part_index = lax.axis_index("tp")
    slots, _ = queries.shape
    k_width = new_keys.shape[1]
    heads_here = H // parts
    offset = mig_dst[0]
    start = (part_index * key_pool.shape[1]).reshape(1)
    visitor, keys_out, values_out = picked(
        page_table, mig_slot, queries, new_keys, new_values, key_pool, value_pool
    )

    def branch(distance):
        def run(visitor, keys_out, values_out):
            back = lax.ppermute(visitor, "rep", route_by(replicas, -distance))
            moved_keys = lax.ppermute(keys_out, "rep", route_by(replicas, distance))
            moved_values = lax.ppermute(values_out, "rep", route_by(replicas, distance))
            own_len = lax.dynamic_slice_in_dim(lengths, here_rep * slots, slots)
            tokens = jnp.concatenate([queries, new_keys, new_values], axis=1)
            tokens = tokens.reshape(slots, -1, DH)
            q_all, mine = shared(mig_slot, back, tokens, heads_here, parts)
            flat = mine[:, heads_here:].reshape(slots, 2 * k_width)
            token_keys = token_rows(flat[:, :k_width], parts, part_index)
            token_values = token_rows(flat[:, k_width:], parts, part_index)
            partials = attended_parts(
                page_table, own_len, start, q_all, key_pool, value_pool, parts
            )
            result, leaver = finished(mig_slot, partials, mine, token_keys, token_values)
            arrived = lax.ppermute(leaver, "rep", route_by(replicas, distance))
            return result, arrived, moved_keys, moved_values

        return run

    result, arrived, moved_keys, moved_values = lax.switch(
        offset - 1,
        [branch(distance) for distance in range(1, replicas)],
        visitor,
        keys_out,
        values_out,
    )
    return placed_results(mig_slot, result, arrived, moved_keys, moved_values)


def leaver_place(slots):
    return min(3, slots - 1)


def slot_at(place, leaving, spot):
    index = place - jnp.where(place > spot, 1, 0)
    other = index + jnp.where(index >= leaving, 1, 0)
    return jnp.where(place == spot, leaving, other)


def serve_kernel(
    distance,
    len_ref,
    mig_ref,
    table_ref,
    queries_ref,
    keys_ref,
    values_ref,
    key_hbm,
    value_hbm,
    out_ref,
    kout_ref,
    vout_ref,
    kpool,
    vpool,
    ksend,
    vsend,
    loose,
    q_ref,
    tokens_ref,
    q_all,
    visit,
    part,
    stats,
    early,
    landed,
    lstats,
    learly,
    row_out,
    row_in,
    flat,
    pool_sems,
    bulk_sems,
    visit_sems,
    share_sems,
    relay_sems,
    early_sems,
    late_sems,
    row_sems,
):
    pages, rows, width = kout_ref.shape
    slots, heads_here = q_ref.shape[:2]
    groups_here = (tokens_ref.shape[1] - heads_here) // 2
    replicas, parts = lax.axis_size("rep"), lax.axis_size("tp")
    rep, me = lax.axis_index("rep"), lax.axis_index("tp")
    spot = leaver_place(slots)
    group = H // KVH
    repeat = heads_here // groups_here
    page_len = rows * parts
    scaling = 1.0 / math.sqrt(DH)
    leaving = mig_ref[rep]
    ahead = lax.rem(rep + distance, replicas)
    behind = lax.rem(rep + replicas - distance, replicas)
    peers = [lax.rem(me + k, parts) for k in range(1, parts)]
    mesh_id = pl.DeviceIdType.MESH

    barrier = pltpu.get_barrier_semaphore()
    for other in (ahead, behind):
        pl.semaphore_signal(barrier, inc=1, device_id={"rep": other}, device_id_type=mesh_id)
    for peer in peers:
        pl.semaphore_signal(barrier, inc=1, device_id={"tp": peer}, device_id_type=mesh_id)

    loads = []
    cuts = pool_sems.shape[1]
    step = kpool.shape[0] // cuts
    for n, (source, target) in enumerate(((key_hbm, kpool), (value_hbm, vpool))):
        for c in range(cuts):
            cut = pl.ds(c * step, step)
            loads.append(
                pltpu.make_async_copy(source.at[cut], target.at[cut], pool_sems.at[n, c])
            )
    for copy in loads:
        copy.start()

    row_of = 0
    for ref in (queries_ref, keys_ref, values_ref):
        whole = ref[...].astype(jnp.float32)
        for h in range(ref.shape[1] // DH):
            loose[:, row_of, :] = whole[:, h * DH : (h + 1) * DH]
            row_of += 1
    for i in range(slots):
        token = loose[slot_at(i, leaving, spot)].astype(q_ref.dtype)
        tokens_ref[i] = token
        q_ref[i] = token[:heads_here]

    pl.semaphore_wait(barrier, parts + 1)

    def remote(source, target, sems, k, device):
        return pltpu.make_async_remote_copy(
            src_ref=source,
            dst_ref=target,
            send_sem=sems.at[0, k],
            recv_sem=sems.at[1, k],
            device_id=device,
            device_id_type=mesh_id,
        )

    visitor = remote(tokens_ref.at[spot], visit, visit_sems, 0, {"rep": behind})
    visitor.start()
    shares = []
    for k, peer in enumerate(peers):
        for n, cut in enumerate((pl.ds(0, spot), pl.ds(spot + 1, slots - spot - 1))):
            if cut.size:
                shares.append(
                    remote(
                        q_ref.at[cut], q_all.at[me, cut], share_sems, 2 * k + n, {"tp": peer}
                    )
                )
    for copy in shares:
        copy.start()
    q_all[me, 0:spot] = q_ref[0:spot]
    q_all[me, spot + 1 :] = q_ref[spot + 1 :]

    for copy in loads[:cuts]:
        copy.wait()
    blank = jnp.zeros((rows, width), ksend.dtype)

    def fill(target, pool):
        @pl.loop(0, pages)
        def _(j):
            page = table_ref[leaving, j]
            target[j] = jnp.where(page >= 0, pool[jnp.maximum(page, 0)], blank)

    fill(ksend, kpool)
    bulk_keys = remote(ksend, kout_ref, bulk_sems, 0, {"rep": ahead})
    bulk_keys.start()
    for copy in loads[cuts:]:
        copy.wait()
    fill(vsend, vpool)
    bulk_values = remote(vsend, vout_ref, bulk_sems, 1, {"rep": ahead})
    bulk_values.start()

    visitor.wait()
    relays = [
        remote(visit.at[pl.ds(0, heads_here)], q_all.at[me, spot], relay_sems, k, {"tp": peer})
        for k, peer in enumerate(peers)
    ]
    for copy in relays:
        copy.start()
    q_all[me, spot] = visit[0:heads_here]
    for copy in shares:
        copy.wait()

    head = lax.broadcasted_iota(jnp.int32, (H, DH), 0) // group
    column = lax.broadcasted_iota(jnp.int32, (heads_here, DH), 1)
    lane = lax.broadcasted_iota(jnp.int32, (H, pages * rows), 1)
    position = (lane // rows) * page_len + lane % rows + me * rows
    stats[...] = jnp.zeros_like(stats)

    early_copies = []
    for k, peer in enumerate(peers):
        early_copies.append(
            remote(part.at[peer, spot], landed.at[k, spot], early_sems, 2 * k, {"tp": peer})
        )
        early_copies.append(
            remote(early.at[peer], learly.at[k], early_sems, 2 * k + 1, {"tp": peer})
        )

    @pl.loop(0, slots)
    def _(i):
        @pl.when(i == spot)
        def _():
            for copy in relays:
                copy.wait()

        slot = slot_at(i, leaving, spot)
        length = len_ref[rep * slots + slot]

        def cached(pool):
            return jnp.concatenate(
                [pool[jnp.maximum(table_ref[slot, j], 0)] for j in range(pages)], axis=0
            )

        q = jnp.concatenate([q_all[t, i].astype(jnp.float32) for t in range(parts)], axis=0)
        spread = jnp.concatenate(
            [jnp.where(head == g, q, 0.0).astype(jnp.bfloat16) for g in range(KVH)], axis=1
        )
        scores = lax.dot_general(
            spread, cached(kpool), (((1,), (1,)), ((), ())), preferred_element_type=jnp.float32
        )
        usable = position < length
        masked = jnp.where(usable, scores * scaling, LOW)
        peak = jnp.max(masked, axis=1, keepdims=True)
        weights = jnp.where(usable, jnp.exp(masked - peak), 0.0)
        total = jnp.sum(weights, axis=1, keepdims=True)
        mixed = jnp.dot(
            weights.astype(jnp.bfloat16), cached(vpool), preferred_element_type=jnp.float32
        )
        own = jnp.concatenate(
            [mixed[g * group : (g + 1) * group, g * DH : (g + 1) * DH] for g in range(KVH)],
            axis=0,
        )
        for t in range(parts):
            cut = slice(t * heads_here, (t + 1) * heads_here)
            part[t, i] = own[cut]
            kept = jnp.where(column == i, peak[cut], stats[t])
            stats[t] = jnp.where(column == i + slots, total[cut], kept)

        @pl.when(i == spot)
        def _():
            early[...] = stats[...]
            for copy in early_copies:
                copy.start()

    late_copies = []
    for k, peer in enumerate(peers):
        for n, cut in enumerate((pl.ds(0, spot), pl.ds(spot + 1, slots - spot - 1))):
            if cut.size:
                late_copies.append(
                    remote(
                        part.at[peer, cut], landed.at[k, cut], late_sems, 3 * k + n, {"tp": peer}
                    )
                )
        late_copies.append(
            remote(stats.at[peer], lstats.at[k], late_sems, 3 * k + 2, {"tp": peer})
        )
    for copy in late_copies:
        copy.start()

    def over_groups(value):
        return jnp.concatenate(
            [jnp.broadcast_to(value[g : g + 1], (repeat, DH)) for g in range(groups_here)],
            axis=0,
        )

    def merged(i, token, rows_of_stats):
        token = token.astype(jnp.float32)
        keys = over_groups(token[heads_here : heads_here + groups_here])
        values = over_groups(token[heads_here + groups_here :])
        fresh = jnp.sum(token[:heads_here] * keys, axis=-1, keepdims=True) * scaling
        top = fresh
        for stat in rows_of_stats:
            top = jnp.maximum(top, stat[:, i : i + 1])
        weight = jnp.exp(fresh - top)
        total = weight
        mixed = weight.astype(jnp.bfloat16).astype(jnp.float32) * values
        for k, stat in enumerate(rows_of_stats):
            scale = jnp.exp(stat[:, i : i + 1] - top)
            block = part[me, i] if k == 0 else landed[k - 1, i]
            total = total + scale * stat[:, slots + i : slots + i + 1]
            mixed = mixed + scale * block
        return mixed / total

    for copy in early_copies:
        copy.wait()
    rows_of_stats = [early[me]] + [learly[k] for k in range(parts - 1)]
    row_out[...] = merged(spot, visit[...], rows_of_stats).astype(row_out.dtype)
    row = remote(row_out, row_in, row_sems, 0, {"rep": ahead})
    row.start()

    for copy in late_copies:
        copy.wait()
    rows_of_stats = [stats[me]] + [lstats[k] for k in range(parts - 1)]
    results = [
        merged(i, tokens_ref[i], rows_of_stats) if i != spot else None for i in range(slots)
    ]
    others = [r for r in results if r is not None]
    row.wait()
    arrived = row_in[...].astype(jnp.float32)
    for i in range(slots):
        before = others[i - 1] if i > 0 else arrived
        after = others[i] if i < slots - 1 else arrived
        value = jnp.where(leaving < i, before, after)
        value = jnp.where(leaving == i, arrived, value)
        for h in range(heads_here):
            flat[i : i + 1, h * DH : (h + 1) * DH] = value[h : h + 1]
    out_ref[...] = flat[...].astype(out_ref.dtype)
    bulk_keys.wait()
    bulk_values.wait()


def served(distance, lengths, mig_slot, table, queries, keys, values, key_pool, value_pool):
    slots, pages = table.shape
    rows, width = key_pool.shape[1:]
    parts = lax.axis_size("tp")
    heads_here = H // parts
    heads_all = heads_here + 2 * keys.shape[1] // DH
    others = parts - 1
    dtype = queries.dtype
    moved = (pages, rows, width)
    part = (slots, heads_here, DH)
    cuts = 2 if key_pool.shape[0] % 2 == 0 else 1
    return pl.pallas_call(
        functools.partial(serve_kernel, distance),
        out_shape=[
            jax.ShapeDtypeStruct(queries.shape, dtype),
            jax.ShapeDtypeStruct(moved, dtype),
            jax.ShapeDtypeStruct(moved, dtype),
        ],
        in_specs=[pl.BlockSpec(memory_space=pltpu.SMEM)] * 3
        + [pl.BlockSpec(memory_space=pltpu.VMEM)] * 3
        + [pl.BlockSpec(memory_space=pltpu.HBM)] * 2,
        out_specs=[pl.BlockSpec(memory_space=pltpu.VMEM)] * 3,
        scratch_shapes=[
            pltpu.VMEM(key_pool.shape, dtype),
            pltpu.VMEM(key_pool.shape, dtype),
            pltpu.VMEM(moved, dtype),
            pltpu.VMEM(moved, dtype),
            pltpu.VMEM((slots, heads_all, DH), jnp.float32),
            pltpu.VMEM(part, dtype),
            pltpu.VMEM((slots, heads_all, DH), dtype),
            pltpu.VMEM((parts,) + part, dtype),
            pltpu.VMEM((heads_all, DH), dtype),
            pltpu.VMEM((parts,) + part, jnp.float32),
            pltpu.VMEM((parts, heads_here, DH), jnp.float32),
            pltpu.VMEM((parts, heads_here, DH), jnp.float32),
            pltpu.VMEM((others,) + part, jnp.float32),
            pltpu.VMEM((others, heads_here, DH), jnp.float32),
            pltpu.VMEM((others, heads_here, DH), jnp.float32),
            pltpu.VMEM((heads_here, DH), dtype),
            pltpu.VMEM((heads_here, DH), dtype),
            pltpu.VMEM((slots, heads_here * DH), jnp.float32),
            pltpu.SemaphoreType.DMA((2, cuts)),
            pltpu.SemaphoreType.DMA((2, 2)),
            pltpu.SemaphoreType.DMA((2, 1)),
            pltpu.SemaphoreType.DMA((2, 2 * others)),
            pltpu.SemaphoreType.DMA((2, others)),
            pltpu.SemaphoreType.DMA((2, 2 * others)),
            pltpu.SemaphoreType.DMA((2, 3 * others)),
            pltpu.SemaphoreType.DMA((2, 1)),
        ],
        compiler_params=pltpu.CompilerParams(
            collective_id=2 + distance, has_side_effects=True, vmem_limit_bytes=32 << 20
        ),
        cost_estimate=pl.CostEstimate(
            flops=4 * H * slots * pages * rows * width,
            bytes_accessed=4 * math.prod(key_pool.shape),
            transcendentals=0,
        ),
    )(lengths, mig_slot, table, queries, keys, values, key_pool, value_pool)


def settle_kernel(result_ref, key_ref, value_ref, out_ref, kout_ref, vout_ref, sems):
    copies = [
        pltpu.make_async_copy(source, target, sems.at[n])
        for n, (source, target) in enumerate(
            ((key_ref, kout_ref), (value_ref, vout_ref), (result_ref, out_ref))
        )
    ]
    for copy in copies:
        copy.start()
    for copy in copies:
        copy.wait()


def settled(*arrays):
    return pl.pallas_call(
        settle_kernel,
        out_shape=[jax.ShapeDtypeStruct(a.shape, a.dtype) for a in arrays],
        in_specs=[pl.BlockSpec(memory_space=pltpu.VMEM)] * 3,
        out_specs=[pl.BlockSpec(memory_space=pltpu.HBM)] * 3,
        scratch_shapes=[pltpu.SemaphoreType.DMA((3,))],
        compiler_params=pltpu.CompilerParams(vmem_limit_bytes=8 << 20),
    )(*arrays)


def swift_body(
    queries, new_keys, new_values, key_pool, value_pool, lengths, page_table, mig_slot, mig_dst
):
    replicas = lax.axis_size("rep")
    results = lax.switch(
        mig_dst[0] - 1,
        [functools.partial(served, distance) for distance in range(1, replicas)],
        lengths,
        mig_slot,
        page_table,
        queries,
        new_keys,
        new_values,
        key_pool,
        value_pool,
    )
    return settled(*results)


def solution(mesh):
    placed = (
        P("rep", "tp"),
        P("rep", "tp"),
        P("rep", "tp"),
        P("rep", "tp", None),
        P("rep", "tp", None),
        P(),
        P("rep", None),
        P(),
        P(),
    )
    swift = KVH % mesh.shape["tp"] == 0
    return jax.shard_map(
        swift_body if swift else body,
        mesh=mesh,
        in_specs=placed,
        out_specs=(P("rep", "tp"), P("rep", "tp", None), P("rep", "tp", None)),
        check_vma=False,
    )
```

profile of v0, /device:TPU:0, one launch (start us, length us, event | category | flops | bytes accessed | tf_op | source)
XLA Modules:
  0.0 46.7 jit_solution(17299514373736214027)
XLA Ops:
  1.3 44.2 %conditional.1 = ((bf16[8,2048]{1,0:T(8,128)(2,1)S(1)}, bf16[12,32,1024]{2,1,0:T(8,128)(2,1)S(1)}, bf16[12,32,1024]{2,1,0:T(8,128)(2,1)S(1)})) conditional(s32[]{:T(128)} %bitcast, (s32[64]{0:T(128)}, s32[8]{0:T(128)}, s32[8,12]{1,0:T(8,128)}, bf16[8,2048]{1,0:T(8,128)(2,1)}, bf16[8,256]{1,0:T(8,128)(2,1)}, ...), branch_computations={%region_0.0_spmd, %region_1.0_spmd, %region_2.0_spmd, %region_3.0_... | conditional | flops 805306368 | bytes 12582920 | solution.py:848
  1.3 44.2 %branch_1_fun.1 = (bf16[8,2048]{1,0:T(8,128)(2,1)S(1)}, bf16[12,32,1024]{2,1,0:T(8,128)(2,1)S(1)}, bf16[12,32,1024]{2,1,0:T(8,128)(2,1)S(1)}) custom-call(s32[64]{0:T(128)} %get-tuple-element.120.len_ref, s32[8]{0:T(128)} %get-tuple-element.121.mig_ref, s32[8,12]{1,0:T(8,128)} %get-tuple-element.122.table_ref, ...), custom_call_target="tpu_custom_call" | custom-call | flops 805306368 | bytes 12582912 | tf_op jit(solution)/shard_map/cond/branch_1_fun/pallas_call | solution.py:770
  45.5 1.2 %shard_map.112 = (bf16[8,2048]{1,0:T(8,128)(2,1)}, bf16[12,32,1024]{2,1,0:T(8,128)(2,1)}, bf16[12,32,1024]{2,1,0:T(8,128)(2,1)}) custom-call(bf16[8,2048]{1,0:T(8,128)(2,1)S(1)} %get-tuple-element.174.result_ref, bf16[12,32,1024]{2,1,0:T(8,128)(2,1)S(1)} %get-tuple-element.175.key_ref, bf16[12,32,1024]{2,1,0:T(8,128)(2,1)S(1)} %get-tuple-element.176.value_ref), custom_call_target="tpu_custom_call" | custom-call | tf_op jit(solution)/shard_map/pallas_call | solution.py:834
where the time goes:
time: 46.9 us; the launch traced here: 46.7 us
  Pallas kernels  45.4 us (97%)
  between operations  1.29 us (3%)
    pallas_call x1, Pallas kernels, served(): pl.pallas_call(functools.partial(serve_kernel, distance), out_shape=[jax....  44.2 us
    pallas_call x1, Pallas kernels, settled(): pl.pallas_call(settle_kernel, out_shape=[jax.ShapeDtypeStruct(a.shape, a....  1.17 us

commit v1 on v0

--- a/solution.py
+++ b/solution.py
@@ -479,6 +479,43 @@
     return min(3, slots - 1)
 
 
+def crossing(replicas, distance):
+    cuts = {}
+    for source in range(replicas):
+        start, end = source // 2, (source + distance) % replicas // 2
+        for chip in range(min(start, end), max(start, end)):
+            cuts.setdefault((chip, end > start), []).append(source)
+    return cuts
+
+
+def paired_sources(replicas, distance):
+    cuts = crossing(replicas, distance).values()
+    most = max(map(len, cuts))
+    busiest = [flows for flows in cuts if len(flows) == most]
+    return [
+        s for s in range(replicas) if any(s in flows and s ^ 1 in flows for flows in busiest)
+    ]
+
+
+def passing(replicas, distance):
+    return sorted(set(sum(crossing(replicas, distance).values(), [])))
+
+
+def room_choices(replicas, distance, pages):
+    if replicas % 2:
+        return [pages]
+    if paired_sources(replicas, distance):
+        return [8, 10, 12]
+    return [pages]
+
+
+def among(index, members):
+    found = index < 0
+    for member in members:
+        found = found | (index == member)
+    return found
+
+
 def slot_at(place, leaving, spot):
     index = place - jnp.where(place > spot, 1, 0)
     other = index + jnp.where(index >= leaving, 1, 0)
@@ -487,21 +524,30 @@
 
 def serve_kernel(
     distance,
+    room,
+    len_hbm,
+    mig_hbm,
+    table_hbm,
+    queries_hbm,
+    keys_hbm,
+    values_hbm,
+    key_hbm,
+    value_hbm,
+    out_ref,
+    kout_ref,
+    vout_ref,
     len_ref,
     mig_ref,
     table_ref,
     queries_ref,
     keys_ref,
     values_ref,
-    key_hbm,
-    value_hbm,
-    out_ref,
-    kout_ref,
-    vout_ref,
     kpool,
     vpool,
     ksend,
     vsend,
+    kguest,
+    vguest,
     loose,
     q_ref,
     tokens_ref,
@@ -515,9 +561,12 @@
     learly,
     row_out,
     row_in,
-    flat,
+    done,
+    ordered,
+    small_sems,
     pool_sems,
     bulk_sems,
+    post_sems,
     visit_sems,
     share_sems,
     relay_sems,
@@ -525,7 +574,7 @@
     late_sems,
     row_sems,
 ):
-    pages, rows, width = kout_ref.shape
+    pages, rows, _ = kout_ref.shape
     slots, heads_here = q_ref.shape[:2]
     groups_here = (tokens_ref.shape[1] - heads_here) // 2
     replicas, parts = lax.axis_size("rep"), lax.axis_size("tp")
@@ -535,18 +584,48 @@
     repeat = heads_here // groups_here
     page_len = rows * parts
     scaling = 1.0 / math.sqrt(DH)
-    leaving = mig_ref[rep]
     ahead = lax.rem(rep + distance, replicas)
     behind = lax.rem(rep + replicas - distance, replicas)
     peers = [lax.rem(me + k, parts) for k in range(1, parts)]
     mesh_id = pl.DeviceIdType.MESH
 
+    alone = not paired_sources(replicas, distance)
+    extra = 0 if alone else pages - room
+    members = paired_sources(replicas, distance) if extra else []
+    sends_paired = among(rep, members)
+    gets_paired = among(behind, members)
+    partner = rep + 1 - 2 * lax.rem(rep, 2)
+    mate = lax.rem(behind + 1 - 2 * lax.rem(behind, 2) + distance, replicas)
+
     barrier = pltpu.get_barrier_semaphore()
+
+    def greet_rep(other):
+        pl.semaphore_signal(barrier, inc=1, device_id={"rep": other}, device_id_type=mesh_id)
+
     for other in (ahead, behind):
-        pl.semaphore_signal(barrier, inc=1, device_id={"rep": other}, device_id_type=mesh_id)
+        greet_rep(other)
     for peer in peers:
         pl.semaphore_signal(barrier, inc=1, device_id={"tp": peer}, device_id_type=mesh_id)
-
+    if extra:
+        greet_rep(partner)
+        if distance % 2:
+            greet_rep(mate)
+
+    smalls = [
+        pltpu.make_async_copy(source, target, small_sems.at[n])
+        for n, (source, target) in enumerate(
+            (
+                (table_hbm, table_ref),
+                (mig_hbm, mig_ref),
+                (len_hbm, len_ref),
+                (queries_hbm, queries_ref),
+                (keys_hbm, keys_ref),
+                (values_hbm, values_ref),
+            )
+        )
+    ]
+    for copy in smalls:
+        copy.start()
     loads = []
     cuts = pool_sems.shape[1]
     step = kpool.shape[0] // cuts
@@ -556,9 +635,12 @@
             loads.append(
                 pltpu.make_async_copy(source.at[cut], target.at[cut], pool_sems.at[n, c])
             )
-    for copy in loads:
+    for copy in loads[:cuts]:
         copy.start()
 
+    for copy in smalls:
+        copy.wait()
+    leaving = mig_ref[rep]
     row_of = 0
     for ref in (queries_ref, keys_ref, values_ref):
         whole = ref[...].astype(jnp.float32)
@@ -570,7 +652,7 @@
         tokens_ref[i] = token
         q_ref[i] = token[:heads_here]
 
-    pl.semaphore_wait(barrier, parts + 1)
+    pl.semaphore_wait(barrier, parts + 1 + (1 + distance % 2 if extra else 0))
 
     def remote(source, target, sems, k, device):
         return pltpu.make_async_remote_copy(
@@ -598,24 +680,62 @@
     q_all[me, 0:spot] = q_ref[0:spot]
     q_all[me, spot + 1 :] = q_ref[spot + 1 :]
 
-    for copy in loads[:cuts]:
-        copy.wait()
-    blank = jnp.zeros((rows, width), ksend.dtype)
+    main = room - extra
+    first = min(2, main)
+    to_ahead, to_partner, to_mate = {"rep": ahead}, {"rep": partner}, {"rep": mate}
+    lanes = ((ksend, kguest, kout_ref), (vsend, vguest, vout_ref))
+
+    def cut_copy(n, kind, low, high):
+        source, _, target = lanes[n]
+        cut = pl.ds(low, high - low)
+        return remote(source.at[cut], target.at[cut], bulk_sems, 2 * kind + n, to_ahead)
+
+    plain = [cut_copy(n, 0, 0, room if alone else pages) for n in range(2)]
+    opening, shared_out, closing, swaps, posts = [], [], [], [], []
+    if extra:
+        if first:
+            opening = [cut_copy(n, 1, 0, first) for n in range(2)]
+        shared_out = [cut_copy(n, 2, main, room) for n in range(2)]
+        if main > first:
+            closing = [cut_copy(n, 3, first, main) for n in range(2)]
+        for n, (source, guest, target) in enumerate(lanes):
+            swaps.append(
+                remote(source.at[pl.ds(room, extra)], guest, bulk_sems, 8 + n, to_partner)
+            )
+            for i in range(extra):
+                posts.append(
+                    remote(
+                        target.at[room - 1 - i],
+                        target.at[room + i],
+                        post_sems,
+                        n * extra + i,
+                        to_mate,
+                    )
+                )
 
     def fill(target, pool):
         @pl.loop(0, pages)
         def _(j):
-            page = table_ref[leaving, j]
-            target[j] = jnp.where(page >= 0, pool[jnp.maximum(page, 0)], blank)
-
-    fill(ksend, kpool)
-    bulk_keys = remote(ksend, kout_ref, bulk_sems, 0, {"rep": ahead})
-    bulk_keys.start()
-    for copy in loads[cuts:]:
-        copy.wait()
-    fill(vsend, vpool)
-    bulk_values = remote(vsend, vout_ref, bulk_sems, 1, {"rep": ahead})
-    bulk_values.start()
+            target[j] = pool[jnp.maximum(table_ref[leaving, j], 0)]
+
+    for n, pool in enumerate((kpool, vpool)):
+        for copy in loads[n * cuts : (n + 1) * cuts]:
+            copy.wait()
+        if n == 0:
+            for copy in loads[cuts:]:
+                copy.start()
+        fill(lanes[n][0], pool)
+        if extra:
+
+            @pl.when(sends_paired)
+            def _():
+                swaps[n].start()
+                if opening:
+                    opening[n].start()
+
+            pl.when(jnp.logical_not(sends_paired))(plain[n].start)
+        else:
+            plain[n].start()
 
     visitor.wait()
     relays = [
@@ -627,6 +747,22 @@
     q_all[me, spot] = visit[0:heads_here]
     for copy in shares:
         copy.wait()
+
+    if extra:
+
+        @pl.when(sends_paired)
+        def _():
+            theirs = len_ref[partner * slots + mig_ref[partner]]
+            for n, (source, guest, _) in enumerate(lanes):
+                swaps[n].wait()
+                for i in range(extra):
+                    spare = room - 1 - i
+                    source[spare] = jnp.where(
+                        theirs > (room + i) * page_len, guest[i], source[spare]
+                    )
+                shared_out[n].start()
+            for copy in closing:
+                copy.start()
 
     head = lax.broadcasted_iota(jnp.int32, (H, DH), 0) // group
     column = lax.broadcasted_iota(jnp.int32, (heads_here, DH), 1)
@@ -711,20 +847,24 @@
         )
 
     def merged(i, token, rows_of_stats):
+        def entry(stat, place):
+            return jnp.sum(jnp.where(column == place, stat, 0.0), axis=1, keepdims=True)
+
         token = token.astype(jnp.float32)
         keys = over_groups(token[heads_here : heads_here + groups_here])
         values = over_groups(token[heads_here + groups_here :])
         fresh = jnp.sum(token[:heads_here] * keys, axis=-1, keepdims=True) * scaling
+        peaks = [entry(stat, i) for stat in rows_of_stats]
         top = fresh
-        for stat in rows_of_stats:
-            top = jnp.maximum(top, stat[:, i : i + 1])
+        for peak in peaks:
+            top = jnp.maximum(top, peak)
         weight = jnp.exp(fresh - top)
         total = weight
         mixed = weight.astype(jnp.bfloat16).astype(jnp.float32) * values
         for k, stat in enumerate(rows_of_stats):
-            scale = jnp.exp(stat[:, i : i + 1] - top)
+            scale = jnp.exp(peaks[k] - top)
             block = part[me, i] if k == 0 else landed[k - 1, i]
-            total = total + scale * stat[:, slots + i : slots + i + 1]
+            total = total + scale * entry(stat, slots + i)
             mixed = mixed + scale * block
         return mixed / total
 
@@ -737,26 +877,65 @@
 
     for copy in late_copies:
         copy.wait()
-    rows_of_stats = [stats[me]] + [lstats[k] for k in range(parts - 1)]
-    results = [
-        merged(i, tokens_ref[i], rows_of_stats) if i != spot else None for i in range(slots)
-    ]
-    others = [r for r in results if r is not None]
+
+    @pl.loop(0, slots - 1)
+    def _(n):
+        i = n + jnp.where(n >= spot, 1, 0)
+        rows_of_stats = [stats[me]] + [lstats[k] for k in range(parts - 1)]
+        done[i] = merged(i, tokens_ref[i], rows_of_stats)
+
+    done[spot] = jnp.zeros(done.shape[1:], done.dtype)
+
+    @pl.loop(0, slots)
+    def _(i):
+        index = i - jnp.where(i > leaving, 1, 0)
+        place = index + jnp.where(index >= spot, 1, 0)
+        ordered[i] = done[jnp.where(i == leaving, spot, place)]
+
+    flat = jnp.concatenate([ordered[:, h, :] for h in range(heads_here)], axis=1)
+    if extra:
+
+        @pl.when(gets_paired)
+        def _():
+            for copy in shared_out:
+                copy.wait_recv()
+            for copy in posts:
+                copy.start()
+
     row.wait()
     arrived = row_in[...].astype(jnp.float32)
-    for i in range(slots):
-        before = others[i - 1] if i > 0 else arrived
-        after = others[i] if i < slots - 1 else arrived
-        value = jnp.where(leaving < i, before, after)
-        value = jnp.where(leaving == i, arrived, value)
-        for h in range(heads_here):
-            flat[i : i + 1, h * DH : (h + 1) * DH] = value[h : h + 1]
-    out_ref[...] = flat[...].astype(out_ref.dtype)
-    bulk_keys.wait()
-    bulk_values.wait()
-
-
-def served(distance, lengths, mig_slot, table, queries, keys, values, key_pool, value_pool):
+    arrived = jnp.concatenate([arrived[h : h + 1] for h in range(heads_here)], axis=1)
+    taken_row = lax.broadcasted_iota(jnp.int32, flat.shape, 0) == leaving
+    out_ref[...] = jnp.where(taken_row, arrived, flat).astype(out_ref.dtype)
+    if not extra:
+        for copy in plain:
+            copy.wait()
+        return
+
+    @pl.when(sends_paired)
+    def _():
+        for copy in opening + shared_out + closing:
+            copy.wait_send()
+
+    @pl.when(gets_paired)
+    def _():
+        for copy in opening + closing:
+            copy.wait_recv()
+        for copy in posts:
+            copy.wait()
+
+    @pl.when(jnp.logical_not(sends_paired))
+    def _():
+        for copy in plain:
+            copy.wait_send()
+
+    @pl.when(jnp.logical_not(gets_paired))
+    def _():
+        for copy in plain:
+            copy.wait_recv()
+
+
+def served(serial, distance, room, lengths, mig_slot, table, queries, keys, values, key_pool, value_pool):
     slots, pages = table.shape
     rows, width = key_pool.shape[1:]
     parts = lax.axis_size("tp")
@@ -767,22 +946,30 @@
     moved = (pages, rows, width)
     part = (slots, heads_here, DH)
     cuts = 2 if key_pool.shape[0] % 2 == 0 else 1
+    extra = pages - room if paired_sources(lax.axis_size("rep"), distance) else 0
+    guests = (max(extra, 1), rows, width)
     return pl.pallas_call(
-        functools.partial(serve_kernel, distance),
+        functools.partial(serve_kernel, distance, room),
         out_shape=[
             jax.ShapeDtypeStruct(queries.shape, dtype),
             jax.ShapeDtypeStruct(moved, dtype),
             jax.ShapeDtypeStruct(moved, dtype),
         ],
-        in_specs=[pl.BlockSpec(memory_space=pltpu.SMEM)] * 3
-        + [pl.BlockSpec(memory_space=pltpu.VMEM)] * 3
-        + [pl.BlockSpec(memory_space=pltpu.HBM)] * 2,
+        in_specs=[pl.BlockSpec(memory_space=pltpu.HBM)] * 8,
         out_specs=[pl.BlockSpec(memory_space=pltpu.VMEM)] * 3,
         scratch_shapes=[
+            pltpu.SMEM(lengths.shape, lengths.dtype),
+            pltpu.SMEM(mig_slot.shape, mig_slot.dtype),
+            pltpu.SMEM(table.shape, table.dtype),
+            pltpu.VMEM(queries.shape, dtype),
+            pltpu.VMEM(keys.shape, dtype),
+            pltpu.VMEM(values.shape, dtype),
             pltpu.VMEM(key_pool.shape, dtype),
             pltpu.VMEM(key_pool.shape, dtype),
             pltpu.VMEM(moved, dtype),
             pltpu.VMEM(moved, dtype),
+            pltpu.VMEM(guests, dtype),
+            pltpu.VMEM(guests, dtype),
             pltpu.VMEM((slots, heads_all, DH), jnp.float32),
             pltpu.VMEM(part, dtype),
             pltpu.VMEM((slots, heads_all, DH), dtype),
@@ -796,9 +983,12 @@
             pltpu.VMEM((others, heads_here, DH), jnp.float32),
             pltpu.VMEM((heads_here, DH), dtype),
             pltpu.VMEM((heads_here, DH), dtype),
-            pltpu.VMEM((slots, heads_here * DH), jnp.float32),
+            pltpu.VMEM(part, jnp.float32),
+            pltpu.VMEM(part, jnp.float32),
+            pltpu.SemaphoreType.DMA((6,)),
             pltpu.SemaphoreType.DMA((2, cuts)),
-            pltpu.SemaphoreType.DMA((2, 2)),
+            pltpu.SemaphoreType.DMA((2, 10)),
+            pltpu.SemaphoreType.DMA((2, max(2 * extra, 1))),
             pltpu.SemaphoreType.DMA((2, 1)),
             pltpu.SemaphoreType.DMA((2, 2 * others)),
             pltpu.SemaphoreType.DMA((2, others)),
@@ -807,7 +997,7 @@
             pltpu.SemaphoreType.DMA((2, 1)),
         ],
         compiler_params=pltpu.CompilerParams(
-            collective_id=2 + distance, has_side_effects=True, vmem_limit_bytes=32 << 20
+            collective_id=2 + serial, has_side_effects=True, vmem_limit_bytes=32 << 20
         ),
         cost_estimate=pl.CostEstimate(
             flops=4 * H * slots * pages * rows * width,
@@ -817,37 +1007,106 @@
     )(lengths, mig_slot, table, queries, keys, values, key_pool, value_pool)
 
 
-def settle_kernel(result_ref, key_ref, value_ref, out_ref, kout_ref, vout_ref, sems):
-    copies = [
-        pltpu.make_async_copy(source, target, sems.at[n])
-        for n, (source, target) in enumerate(
-            ((key_ref, kout_ref), (value_ref, vout_ref), (result_ref, out_ref))
-        )
-    ]
-    for copy in copies:
-        copy.start()
-    for copy in copies:
-        copy.wait()
-
-
-def settled(*arrays):
+def settle_kernel(
+    live_ref,
+    result_ref,
+    key_ref,
+    value_ref,
+    out_ref,
+    kout_ref,
+    vout_ref,
+    blank,
+    result_sem,
+    page_sems,
+):
+    pages = key_ref.shape[0]
+    live = live_ref[0]
+    lanes = ((key_ref, kout_ref), (value_ref, vout_ref))
+    result = pltpu.make_async_copy(result_ref, out_ref, result_sem)
+    result.start()
+    blank[...] = jnp.zeros_like(blank)
+    for j in range(pages):
+        for n, (origin, target) in enumerate(lanes):
+            spot = target.at[j]
+            pl.when(j < live)(pltpu.make_async_copy(origin.at[j], spot, page_sems.at[n]).start)
+            pl.when(j >= live)(pltpu.make_async_copy(blank, spot, page_sems.at[n]).start)
+    for n, (origin, target) in enumerate(lanes):
+        pltpu.make_async_copy(origin, target, page_sems.at[n]).wait()
+    result.wait()
+
+
+def settled(live, *arrays):
+    rows, width = arrays[1].shape[1:]
     return pl.pallas_call(
         settle_kernel,
         out_shape=[jax.ShapeDtypeStruct(a.shape, a.dtype) for a in arrays],
-        in_specs=[pl.BlockSpec(memory_space=pltpu.VMEM)] * 3,
+        in_specs=[pl.BlockSpec(memory_space=pltpu.SMEM)]
+        + [pl.BlockSpec(memory_space=pltpu.VMEM)] * 3,
         out_specs=[pl.BlockSpec(memory_space=pltpu.HBM)] * 3,
-        scratch_shapes=[pltpu.SemaphoreType.DMA((3,))],
+        scratch_shapes=[
+            pltpu.VMEM((rows, width), arrays[1].dtype),
+            pltpu.SemaphoreType.DMA,
+            pltpu.SemaphoreType.DMA((2,)),
+        ],
         compiler_params=pltpu.CompilerParams(vmem_limit_bytes=8 << 20),
-    )(*arrays)
+    )(live, *arrays)
+
+
+def branch_plans(replicas, pages):
+    return [
+        [(distance, room) for room in room_choices(replicas, distance, pages)]
+        for distance in range(1, replicas)
+    ]
+
+
+def choose_kernel(page_len, pages, len_ref, mig_ref, dst_ref, out_ref, live_ref):
+    replicas = mig_ref.shape[0]
+    slots = len_ref.shape[0] // replicas
+
+    def need(source):
+        length = len_ref[source * slots + mig_ref[source]]
+        return lax.div(length + (page_len - 1), page_len)
+
+    needs = [need(source) for source in range(replicas)]
+    distance = dst_ref[0]
+    index, base = jnp.int32(0), 0
+    for step, plans in enumerate(branch_plans(replicas, pages), start=1):
+        place = jnp.int32(base)
+        if len(plans) > 1:
+            worst = jnp.int32(0)
+            members = paired_sources(replicas, step)
+            for source in members[::2]:
+                worst = jnp.maximum(worst, needs[source] + needs[source + 1])
+            for source in [] if members else passing(replicas, step):
+                worst = jnp.maximum(worst, 2 * needs[source])
+            for _, room in plans[:-1]:
+                place = place + jnp.where(worst > 2 * room, 1, 0)
+        index = jnp.where(distance == step, place, index)
+        base += len(plans)
+    out_ref[0] = index
+    live_ref[0] = need(lax.rem(lax.axis_index("rep") + replicas - distance, replicas))
+
+
+def chosen(page_len, pages, lengths, mig_slot, mig_dst):
+    return pl.pallas_call(
+        functools.partial(choose_kernel, page_len, pages),
+        out_shape=[pltpu.SMEM((1,), jnp.int32)] * 2,
+        in_specs=[pl.BlockSpec(memory_space=pltpu.SMEM)] * 3,
+        out_specs=[pl.BlockSpec(memory_space=pltpu.SMEM)] * 2,
+    )(lengths, mig_slot, mig_dst)
 
 
 def swift_body(
     queries, new_keys, new_values, key_pool, value_pool, lengths, page_table, mig_slot, mig_dst
 ):
     replicas = lax.axis_size("rep")
+    pages = page_table.shape[1]
+    page_len = key_pool.shape[1] * lax.axis_size("tp")
+    plans = [plan for group in branch_plans(replicas, pages) for plan in group]
+    index, live = chosen(page_len, pages, lengths, mig_slot, mig_dst)
     results = lax.switch(
-        mig_dst[0] - 1,
-        [functools.partial(served, distance) for distance in range(1, replicas)],
+        index[0],
+        [functools.partial(served, n, *plan) for n, plan in enumerate(plans)],
         lengths,
         mig_slot,
         page_table,
@@ -857,7 +1116,7 @@
         key_pool,
         value_pool,
     )
-    return settled(*results)
+    return settled(live, *results)
 
 
 def solution(mesh):

time: 46.9 us -> 46.7 us (level)
    pallas_call x1 -> x2, Pallas kernels: 44.2 us -> 44.2 us  [the longest x1 43.5 us: served(): pl.pallas_call(functools.partial(serve_kernel, distance, room), out_shape...]
where the time goes in v1:
time: 46.7 us; the launch traced here: 46.5 us
  Pallas kernels  45.4 us (97%)
  between operations  0.83 us (2%)
    pallas_call x1, Pallas kernels, served(): pl.pallas_call(functools.partial(serve_kernel, distance, room), out_shape...  43.5 us
    pallas_call x1, Pallas kernels, settled(): pl.pallas_call(settle_kernel, out_shape=[jax.ShapeDtypeStruct(a.shape, a....  1.15 us

profile of v1, /device:TPU:0, one launch (start us, length us, event | category | flops | bytes accessed | tf_op | source)
XLA Modules:
  0.0 46.5 jit_solution(1306445370759210299)
XLA Ops:
  0.6 0.7 %shard_map.112 = (s32[1]{0:T(128)S(4)}, s32[1]{0:T(128)S(4)}) custom-call(s32[64]{0:T(128)} %len_ref.1, s32[8]{0:T(128)} %mig_ref.1, s32[8]{0:T(128)} %dst_ref.1), custom_call_target="tpu_custom_call" | custom-call | tf_op jit(solution)/shard_map/pallas_call | solution.py:1091
  1.4 43.8 %conditional.1 = ((bf16[8,2048]{1,0:T(8,128)(2,1)S(1)}, bf16[12,32,1024]{2,1,0:T(8,128)(2,1)S(1)}, bf16[12,32,1024]{2,1,0:T(8,128)(2,1)S(1)})) conditional(s32[]{:T(128)} %bitcast, (s32[64]{0:T(128)}, s32[8]{0:T(128)}, s32[8,12]{1,0:T(8,128)}, bf16[8,2048]{1,0:T(8,128)(2,1)}, bf16[8,256]{1,0:T(8,128)(2,1)}, ...), branch_computations={%region_0.0_spmd, %region_1.0_spmd, %region_2.0_spmd, %region_3.0_... | conditional | flops 805306368 | bytes 12582920 | solution.py:1107
  1.4 43.5 %branch_3_fun.1 = (bf16[8,2048]{1,0:T(8,128)(2,1)S(1)}, bf16[12,32,1024]{2,1,0:T(8,128)(2,1)S(1)}, bf16[12,32,1024]{2,1,0:T(8,128)(2,1)S(1)}) custom-call(s32[64]{0:T(128)} %get-tuple-element.296.len_hbm, s32[8]{0:T(128)} %get-tuple-element.297.mig_hbm, s32[8,12]{1,0:T(8,128)} %get-tuple-element.298.table_hbm, ...), custom_call_target="tpu_custom_call" | custom-call | flops 805306368 | bytes 12582912 | tf_op jit(solution)/shard_map/cond/branch_3_fun/pallas_call | solution.py:951
  45.2 1.2 %shard_map.113 = (bf16[8,2048]{1,0:T(8,128)(2,1)}, bf16[12,32,1024]{2,1,0:T(8,128)(2,1)}, bf16[12,32,1024]{2,1,0:T(8,128)(2,1)}) custom-call(s32[1]{0:T(128)S(4)} %get-tuple-element.416.live_ref, bf16[8,2048]{1,0:T(8,128)(2,1)S(1)} %get-tuple-element.418.result_ref, bf16[12,32,1024]{2,1,0:T(8,128)(2,1)S(1)} %get-tuple-element.419.key_ref, ...), custom_call_target="tpu_custom_call" | custom-call | tf_op jit(solution)/shard_map/pallas_call | solution.py:1040

commit v2 on v1

--- a/solution.py
+++ b/solution.py
@@ -497,16 +497,32 @@
     ]
 
 
-def passing(replicas, distance):
-    return sorted(set(sum(crossing(replicas, distance).values(), [])))
-
-
-def room_choices(replicas, distance, pages):
-    if replicas % 2:
-        return [pages]
-    if paired_sources(replicas, distance):
-        return [8, 10, 12]
-    return [pages]
+def lone_sources(replicas, distance):
+    cuts = crossing(replicas, distance).values()
+    most = max(map(len, cuts))
+    members = paired_sources(replicas, distance)
+    return [
+        s
+        for s in range(replicas)
+        if s not in members and any(s in flows and len(flows) == most for flows in cuts)
+    ]
+
+
+def branch_plans(replicas, pages):
+    plans = []
+    for distance in range(1, replicas):
+        rooms, singles = [pages], [pages]
+        if replicas % 2 == 0:
+            low, mid = pages * 2 // 3, pages * 5 // 6
+            paired = paired_sources(replicas, distance)
+            if paired:
+                rooms = [low, mid, pages]
+            if 2 * distance == replicas:
+                rooms.append(pages * 3 // 4)
+            if lone_sources(replicas, distance):
+                singles = [low, pages] if paired else [low, mid, pages]
+        plans.append((distance, sorted(set(rooms)), sorted(set(singles))))
+    return plans
 
 
 def among(index, members):
@@ -525,6 +541,7 @@
 def serve_kernel(
     distance,
     room,
+    single,
     len_hbm,
     mig_hbm,
     table_hbm,
@@ -552,12 +569,11 @@
     q_ref,
     tokens_ref,
     q_all,
+    q_visit,
     visit,
     part,
-    stats,
     early,
     landed,
-    lstats,
     learly,
     row_out,
     row_in,
@@ -589,11 +605,16 @@
     peers = [lax.rem(me + k, parts) for k in range(1, parts)]
     mesh_id = pl.DeviceIdType.MESH
 
-    alone = not paired_sources(replicas, distance)
-    extra = 0 if alone else pages - room
+    extra = pages - room
     members = paired_sources(replicas, distance) if extra else []
-    sends_paired = among(rep, members)
-    gets_paired = among(behind, members)
+    lone = lone_sources(replicas, distance) if single < pages else []
+    rest = [s for s in range(replicas) if s not in members and s not in lone]
+
+    def when(index, group):
+        if len(group) == replicas:
+            return lambda run: run()
+        return pl.when(among(index, group)) if group else lambda run: None
+
     partner = rep + 1 - 2 * lax.rem(rep, 2)
     mate = lax.rem(behind + 1 - 2 * lax.rem(behind, 2) + distance, replicas)
 
@@ -652,6 +673,16 @@
         tokens_ref[i] = token
         q_ref[i] = token[:heads_here]
 
+    def fill(target, pool):
+        @pl.loop(0, pages)
+        def _(j):
+            target[j] = pool[jnp.maximum(table_ref[leaving, j], 0)]
+
+    for copy in loads[:cuts]:
+        copy.wait()
+    for copy in loads[cuts:]:
+        copy.start()
+    fill(ksend, kpool)
     pl.semaphore_wait(barrier, parts + 1 + (1 + distance % 2 if extra else 0))
 
     def remote(source, target, sems, k, device):
@@ -666,19 +697,9 @@
 
     visitor = remote(tokens_ref.at[spot], visit, visit_sems, 0, {"rep": behind})
     visitor.start()
-    shares = []
-    for k, peer in enumerate(peers):
-        for n, cut in enumerate((pl.ds(0, spot), pl.ds(spot + 1, slots - spot - 1))):
-            if cut.size:
-                shares.append(
-                    remote(
-                        q_ref.at[cut], q_all.at[me, cut], share_sems, 2 * k + n, {"tp": peer}
-                    )
-                )
-    for copy in shares:
-        copy.start()
-    q_all[me, 0:spot] = q_ref[0:spot]
-    q_all[me, spot + 1 :] = q_ref[spot + 1 :]
+    shares = [
+        remote(q_ref, q_all.at[me], share_sems, k, {"tp": peer}) for k, peer in enumerate(peers)
+    ]
 
     main = room - extra
     first = min(2, main)
@@ -690,7 +711,8 @@
         cut = pl.ds(low, high - low)
         return remote(source.at[cut], target.at[cut], bulk_sems, 2 * kind + n, to_ahead)
 
-    plain = [cut_copy(n, 0, 0, room if alone else pages) for n in range(2)]
+    plain = [cut_copy(n, 0, 0, pages) for n in range(2)] if rest else []
+    short = [cut_copy(n, 4, 0, single) for n in range(2)] if lone else []
     opening, shared_out, closing, swaps, posts = [], [], [], [], []
     if extra:
         if first:
@@ -700,7 +722,7 @@
             closing = [cut_copy(n, 3, first, main) for n in range(2)]
         for n, (source, guest, target) in enumerate(lanes):
             swaps.append(
-                remote(source.at[pl.ds(room, extra)], guest, bulk_sems, 8 + n, to_partner)
+                remote(source.at[pl.ds(room, extra)], guest, bulk_sems, 10 + n, to_partner)
             )
             for i in range(extra):
                 posts.append(
@@ -713,71 +735,61 @@
                     )
                 )
 
-    def fill(target, pool):
-        @pl.loop(0, pages)
-        def _(j):
-            target[j] = pool[jnp.maximum(table_ref[leaving, j], 0)]
-
-    for n, pool in enumerate((kpool, vpool)):
-        for copy in loads[n * cuts : (n + 1) * cuts]:
-            copy.wait()
-        if n == 0:
-            for copy in loads[cuts:]:
-                copy.start()
-        fill(lanes[n][0], pool)
-        if extra:
-
-            @pl.when(sends_paired)
-            def _():
-                swaps[n].start()
-                if opening:
-                    opening[n].start()
-
-            pl.when(jnp.logical_not(sends_paired))(plain[n].start)
-        else:
-            plain[n].start()
+    def send(n):
+        @when(rep, members)
+        def _():
+            swaps[n].start()
+            if opening:
+                opening[n].start()
+
+        when(rep, lone)(lambda: short[n].start())
+        when(rep, rest)(lambda: plain[n].start())
+
+    send(0)
+    for copy in shares:
+        copy.start()
+    q_all[me] = q_ref[...]
+    for copy in loads[cuts:]:
+        copy.wait()
+    fill(vsend, vpool)
+    send(1)
 
     visitor.wait()
     relays = [
-        remote(visit.at[pl.ds(0, heads_here)], q_all.at[me, spot], relay_sems, k, {"tp": peer})
+        remote(visit.at[pl.ds(0, heads_here)], q_visit.at[me], relay_sems, k, {"tp": peer})
         for k, peer in enumerate(peers)
     ]
     for copy in relays:
         copy.start()
-    q_all[me, spot] = visit[0:heads_here]
+    q_visit[me] = visit[0:heads_here]
     for copy in shares:
         copy.wait()
 
-    if extra:
-
-        @pl.when(sends_paired)
-        def _():
-            theirs = len_ref[partner * slots + mig_ref[partner]]
-            for n, (source, guest, _) in enumerate(lanes):
-                swaps[n].wait()
-                for i in range(extra):
-                    spare = room - 1 - i
-                    source[spare] = jnp.where(
-                        theirs > (room + i) * page_len, guest[i], source[spare]
-                    )
-                shared_out[n].start()
-            for copy in closing:
-                copy.start()
+    @when(rep, members)
+    def _():
+        theirs = len_ref[partner * slots + mig_ref[partner]]
+        for n, (source, guest, _) in enumerate(lanes):
+            swaps[n].wait()
+
+            @pl.loop(0, extra)
+            def _(i):
+                spare = room - 1 - i
+                guested = theirs > (room + i) * page_len
+                source[spare] = jnp.where(guested, guest[i], source[spare])
+
+            shared_out[n].start()
+        for copy in closing:
+            copy.start()
 
     head = lax.broadcasted_iota(jnp.int32, (H, DH), 0) // group
     column = lax.broadcasted_iota(jnp.int32, (heads_here, DH), 1)
     lane = lax.broadcasted_iota(jnp.int32, (H, pages * rows), 1)
     position = (lane // rows) * page_len + lane % rows + me * rows
-    stats[...] = jnp.zeros_like(stats)
-
-    early_copies = []
-    for k, peer in enumerate(peers):
-        early_copies.append(
-            remote(part.at[peer, spot], landed.at[k, spot], early_sems, 2 * k, {"tp": peer})
-        )
-        early_copies.append(
-            remote(early.at[peer], learly.at[k], early_sems, 2 * k + 1, {"tp": peer})
-        )
+    part[:, slots] = jnp.zeros((parts, heads_here, DH), part.dtype)
+    early_copies = [
+        remote(early.at[peer], learly.at[k], early_sems, k, {"tp": peer})
+        for k, peer in enumerate(peers)
+    ]
 
     @pl.loop(0, slots)
     def _(i):
@@ -785,6 +797,8 @@
         def _():
             for copy in relays:
                 copy.wait()
+            for t in range(parts):
+                q_all[t, spot] = q_visit[t]
 
         slot = slot_at(i, leaving, spot)
         length = len_ref[rep * slots + slot]
@@ -816,27 +830,20 @@
         for t in range(parts):
             cut = slice(t * heads_here, (t + 1) * heads_here)
             part[t, i] = own[cut]
-            kept = jnp.where(column == i, peak[cut], stats[t])
-            stats[t] = jnp.where(column == i + slots, total[cut], kept)
+            kept = jnp.where(column == i, peak[cut], part[t, slots])
+            part[t, slots] = jnp.where(column == i + slots, total[cut], kept)
 
         @pl.when(i == spot)
         def _():
-            early[...] = stats[...]
+            early[:, 0] = part[:, spot]
+            early[:, 1] = part[:, slots]
             for copy in early_copies:
                 copy.start()
 
-    late_copies = []
-    for k, peer in enumerate(peers):
-        for n, cut in enumerate((pl.ds(0, spot), pl.ds(spot + 1, slots - spot - 1))):
-            if cut.size:
-                late_copies.append(
-                    remote(
-                        part.at[peer, cut], landed.at[k, cut], late_sems, 3 * k + n, {"tp": peer}
-                    )
-                )
-        late_copies.append(
-            remote(stats.at[peer], lstats.at[k], late_sems, 3 * k + 2, {"tp": peer})
-        )
+    late_copies = [
+        remote(part.at[peer], landed.at[k], late_sems, k, {"tp": peer})
+        for k, peer in enumerate(peers)
+    ]
     for copy in late_copies:
         copy.start()
 
@@ -846,7 +853,7 @@
             axis=0,
         )
 
-    def merged(i, token, rows_of_stats):
+    def merged(i, token, blocks, rows_of_stats):
         def entry(stat, place):
             return jnp.sum(jnp.where(column == place, stat, 0.0), axis=1, keepdims=True)
 
@@ -863,15 +870,15 @@
         mixed = weight.astype(jnp.bfloat16).astype(jnp.float32) * values
         for k, stat in enumerate(rows_of_stats):
             scale = jnp.exp(peaks[k] - top)
-            block = part[me, i] if k == 0 else landed[k - 1, i]
             total = total + scale * entry(stat, slots + i)
-            mixed = mixed + scale * block
+            mixed = mixed + scale * blocks[k]
         return mixed / total
 
     for copy in early_copies:
         copy.wait()
-    rows_of_stats = [early[me]] + [learly[k] for k in range(parts - 1)]
-    row_out[...] = merged(spot, visit[...], rows_of_stats).astype(row_out.dtype)
+    blocks = [early[me, 0]] + [learly[k, 0] for k in range(parts - 1)]
+    rows_of_stats = [early[me, 1]] + [learly[k, 1] for k in range(parts - 1)]
+    row_out[...] = merged(spot, visit[...], blocks, rows_of_stats).astype(row_out.dtype)
     row = remote(row_out, row_in, row_sems, 0, {"rep": ahead})
     row.start()
 
@@ -881,8 +888,9 @@
     @pl.loop(0, slots - 1)
     def _(n):
         i = n + jnp.where(n >= spot, 1, 0)
-        rows_of_stats = [stats[me]] + [lstats[k] for k in range(parts - 1)]
-        done[i] = merged(i, tokens_ref[i], rows_of_stats)
+        blocks = [part[me, i]] + [landed[k, i] for k in range(parts - 1)]
+        rows_of_stats = [part[me, slots]] + [landed[k, slots] for k in range(parts - 1)]
+        done[i] = merged(i, tokens_ref[i], blocks, rows_of_stats)
 
     done[spot] = jnp.zeros(done.shape[1:], done.dtype)
 
@@ -893,49 +901,34 @@
         ordered[i] = done[jnp.where(i == leaving, spot, place)]
 
     flat = jnp.concatenate([ordered[:, h, :] for h in range(heads_here)], axis=1)
-    if extra:
-
-        @pl.when(gets_paired)
-        def _():
-            for copy in shared_out:
-                copy.wait_recv()
-            for copy in posts:
-                copy.start()
+
+    @when(behind, members)
+    def _():
+        for copy in shared_out:
+            copy.wait_recv()
+        for copy in posts:
+            copy.start()
 
     row.wait()
     arrived = row_in[...].astype(jnp.float32)
     arrived = jnp.concatenate([arrived[h : h + 1] for h in range(heads_here)], axis=1)
     taken_row = lax.broadcasted_iota(jnp.int32, flat.shape, 0) == leaving
     out_ref[...] = jnp.where(taken_row, arrived, flat).astype(out_ref.dtype)
-    if not extra:
-        for copy in plain:
-            copy.wait()
-        return
-
-    @pl.when(sends_paired)
-    def _():
-        for copy in opening + shared_out + closing:
-            copy.wait_send()
-
-    @pl.when(gets_paired)
-    def _():
-        for copy in opening + closing:
-            copy.wait_recv()
-        for copy in posts:
-            copy.wait()
-
-    @pl.when(jnp.logical_not(sends_paired))
-    def _():
-        for copy in plain:
-            copy.wait_send()
-
-    @pl.when(jnp.logical_not(gets_paired))
-    def _():
-        for copy in plain:
-            copy.wait_recv()
-
-
-def served(serial, distance, room, lengths, mig_slot, table, queries, keys, values, key_pool, value_pool):
+
+    def settle_all(copies, name):
+        for copy in copies:
+            getattr(copy, name)()
+
+    sends = ((members, opening + shared_out + closing), (lone, short), (rest, plain))
+    gets = ((members, opening + closing), (lone, short), (rest, plain))
+    for group, copies in sends:
+        when(rep, group)(functools.partial(settle_all, copies, "wait_send"))
+    for group, copies in gets:
+        when(behind, group)(functools.partial(settle_all, copies, "wait_recv"))
+    when(behind, members)(functools.partial(settle_all, posts, "wait"))
+
+
+def served(serial, distance, room, single, lengths, mig_slot, table, queries, keys, values, key_pool, value_pool):
     slots, pages = table.shape
     rows, width = key_pool.shape[1:]
     parts = lax.axis_size("tp")
@@ -946,10 +939,10 @@
     moved = (pages, rows, width)
     part = (slots, heads_here, DH)
     cuts = 2 if key_pool.shape[0] % 2 == 0 else 1
-    extra = pages - room if paired_sources(lax.axis_size("rep"), distance) else 0
+    extra = pages - room
     guests = (max(extra, 1), rows, width)
     return pl.pallas_call(
-        functools.partial(serve_kernel, distance, room),
+        functools.partial(serve_kernel, distance, room, single),
         out_shape=[
             jax.ShapeDtypeStruct(queries.shape, dtype),
             jax.ShapeDtypeStruct(moved, dtype),
@@ -974,26 +967,25 @@
             pltpu.VMEM(part, dtype),
             pltpu.VMEM((slots, heads_all, DH), dtype),
             pltpu.VMEM((parts,) + part, dtype),
+            pltpu.VMEM((parts, heads_here, DH), dtype),
             pltpu.VMEM((heads_all, DH), dtype),
-            pltpu.VMEM((parts,) + part, jnp.float32),
-            pltpu.VMEM((parts, heads_here, DH), jnp.float32),
-            pltpu.VMEM((parts, heads_here, DH), jnp.float32),
-            pltpu.VMEM((others,) + part, jnp.float32),
-            pltpu.VMEM((others, heads_here, DH), jnp.float32),
-            pltpu.VMEM((others, heads_here, DH), jnp.float32),
+            pltpu.VMEM((parts, slots + 1, heads_here, DH), jnp.float32),
+            pltpu.VMEM((parts, 2, heads_here, DH), jnp.float32),
+            pltpu.VMEM((others, slots + 1, heads_here, DH), jnp.float32),
+            pltpu.VMEM((others, 2, heads_here, DH), jnp.float32),
             pltpu.VMEM((heads_here, DH), dtype),
             pltpu.VMEM((heads_here, DH), dtype),
             pltpu.VMEM(part, jnp.float32),
             pltpu.VMEM(part, jnp.float32),
             pltpu.SemaphoreType.DMA((6,)),
             pltpu.SemaphoreType.DMA((2, cuts)),
-            pltpu.SemaphoreType.DMA((2, 10)),
+            pltpu.SemaphoreType.DMA((2, 12 if extra else 10)),
             pltpu.SemaphoreType.DMA((2, max(2 * extra, 1))),
             pltpu.SemaphoreType.DMA((2, 1)),
-            pltpu.SemaphoreType.DMA((2, 2 * others)),
             pltpu.SemaphoreType.DMA((2, others)),
-            pltpu.SemaphoreType.DMA((2, 2 * others)),
-            pltpu.SemaphoreType.DMA((2, 3 * others)),
+            pltpu.SemaphoreType.DMA((2, others)),
+            pltpu.SemaphoreType.DMA((2, others)),
+            pltpu.SemaphoreType.DMA((2, others)),
             pltpu.SemaphoreType.DMA((2, 1)),
         ],
         compiler_params=pltpu.CompilerParams(
@@ -1052,13 +1044,6 @@
     )(live, *arrays)
 
 
-def branch_plans(replicas, pages):
-    return [
-        [(distance, room) for room in room_choices(replicas, distance, pages)]
-        for distance in range(1, replicas)
-    ]
-
-
 def choose_kernel(page_len, pages, len_ref, mig_ref, dst_ref, out_ref, live_ref):
     replicas = mig_ref.shape[0]
     slots = len_ref.shape[0] // replicas
@@ -1070,19 +1055,20 @@
     needs = [need(source) for source in range(replicas)]
     distance = dst_ref[0]
     index, base = jnp.int32(0), 0
-    for step, plans in enumerate(branch_plans(replicas, pages), start=1):
+    for step, rooms, singles in branch_plans(replicas, pages):
+        most = jnp.int32(0)
+        for source in paired_sources(replicas, step)[::2] if len(rooms) > 1 else []:
+            most = jnp.maximum(most, needs[source] + needs[source + 1])
+        longest = jnp.int32(0)
+        for source in lone_sources(replicas, step) if len(singles) > 1 else []:
+            longest = jnp.maximum(longest, needs[source])
         place = jnp.int32(base)
-        if len(plans) > 1:
-            worst = jnp.int32(0)
-            members = paired_sources(replicas, step)
-            for source in members[::2]:
-                worst = jnp.maximum(worst, needs[source] + needs[source + 1])
-            for source in [] if members else passing(replicas, step):
-                worst = jnp.maximum(worst, 2 * needs[source])
-            for _, room in plans[:-1]:
-                place = place + jnp.where(worst > 2 * room, 1, 0)
+        for room in rooms[:-1]:
+            place = place + jnp.where(most > 2 * room, len(singles), 0)
+        for single in singles[:-1]:
+            place = place + jnp.where(longest > single, 1, 0)
         index = jnp.where(distance == step, place, index)
-        base += len(plans)
+        base += len(rooms) * len(singles)
     out_ref[0] = index
     live_ref[0] = need(lax.rem(lax.axis_index("rep") + replicas - distance, replicas))
 
@@ -1102,7 +1088,12 @@
     replicas = lax.axis_size("rep")
     pages = page_table.shape[1]
     page_len = key_pool.shape[1] * lax.axis_size("tp")
-    plans = [plan for group in branch_plans(replicas, pages) for plan in group]
+    plans = [
+        (distance, room, single)
+        for distance, rooms, singles in branch_plans(replicas, pages)
+        for room in rooms
+        for single in singles
+    ]
     index, live = chosen(page_len, pages, lengths, mig_slot, mig_dst)
     results = lax.switch(
         index[0],

time: 46.7 us -> 46.5 us (level)
  no operation moved by 1% of the time
where the time goes in v2:
time: 46.5 us; the launch traced here: 46.3 us
  Pallas kernels  45.3 us (97%)
  between operations  0.81 us (2%)
    pallas_call x1, Pallas kernels, served(): pl.pallas_call(functools.partial(serve_kernel, distance, room, single), o...  43.3 us
    pallas_call x1, Pallas kernels, settled(): pl.pallas_call(settle_kernel, out_shape=[jax.ShapeDtypeStruct(a.shape, a....  1.15 us

profile of v2, /device:TPU:0, one launch (start us, length us, event | category | flops | bytes accessed | tf_op | source)
XLA Modules:
  0.0 46.3 jit_solution(10715403288445136519)
XLA Ops:
  0.6 0.8 %shard_map.112 = (s32[1]{0:T(128)S(4)}, s32[1]{0:T(128)S(4)}) custom-call(s32[64]{0:T(128)} %len_ref.1, s32[8]{0:T(128)} %mig_ref.1, s32[8]{0:T(128)} %dst_ref.1), custom_call_target="tpu_custom_call" | custom-call | tf_op jit(solution)/shard_map/pallas_call | solution.py:1077
  1.4 43.6 %conditional.1 = ((bf16[8,2048]{1,0:T(8,128)(2,1)S(1)}, bf16[12,32,1024]{2,1,0:T(8,128)(2,1)S(1)}, bf16[12,32,1024]{2,1,0:T(8,128)(2,1)S(1)})) conditional(s32[]{:T(128)} %bitcast, (s32[64]{0:T(128)}, s32[8]{0:T(128)}, s32[8,12]{1,0:T(8,128)}, bf16[8,2048]{1,0:T(8,128)(2,1)}, bf16[8,256]{1,0:T(8,128)(2,1)}, ...), branch_computations={%region_0.0_spmd, %region_1.0_spmd, %region_2.0_spmd, %region_3.0_... | conditional | flops 805306368 | bytes 12582920 | solution.py:1098
  1.4 43.3 %branch_5_fun.1 = (bf16[8,2048]{1,0:T(8,128)(2,1)S(1)}, bf16[12,32,1024]{2,1,0:T(8,128)(2,1)S(1)}, bf16[12,32,1024]{2,1,0:T(8,128)(2,1)S(1)}) custom-call(s32[64]{0:T(128)} %get-tuple-element.488.len_hbm, s32[8]{0:T(128)} %get-tuple-element.489.mig_hbm, s32[8,12]{1,0:T(8,128)} %get-tuple-element.490.table_hbm, ...), custom_call_target="tpu_custom_call" | custom-call | flops 805306368 | bytes 12582912 | tf_op jit(solution)/shard_map/cond/branch_5_fun/pallas_call | solution.py:944
  45.0 1.2 %shard_map.113 = (bf16[8,2048]{1,0:T(8,128)(2,1)}, bf16[12,32,1024]{2,1,0:T(8,128)(2,1)}, bf16[12,32,1024]{2,1,0:T(8,128)(2,1)}) custom-call(s32[1]{0:T(128)S(4)} %get-tuple-element.680.live_ref, bf16[8,2048]{1,0:T(8,128)(2,1)S(1)} %get-tuple-element.682.result_ref, bf16[12,32,1024]{2,1,0:T(8,128)(2,1)S(1)} %get-tuple-element.683.key_ref, ...), custom_call_target="tpu_custom_call" | custom-call | tf_op jit(solution)/shard_map/pallas_call | solution.py:1032
